TPU v7x, 32 devices: a whole 2x2x4 slice. The times are simulated.
32 devices in a mesh: sky: 2 (over y), ma: 4 (over z), freq: 2 (over x), pol: 2 (over core).
Axes of the slice: x: 2, y: 2, z: 4, core: 2. Of those that a mesh axis runs over, the one named last changes fastest.
Arguments:
- alm: bfloat16 [2, 2, 1024, 4, 1024], P(None, 'freq', ('ma', 'pol'), None, 'sky'), parts along dimension 4, may hold values from -6 to 6
- beam: bfloat16 [4, 2, 2, 1024, 1024], P('ma', 'freq', None, 'pol'), may hold values from -0.1875 to 0.1875
- m_table: int32 [4], P('ma'), may hold values from 0 to 511, as said below
- chan_mask: int32 [2], P('freq'), may hold values from 0 to 1, as said below
- noise: float32 [2, 1024], P('freq', 'pol'), may hold values from 0.5 to 4
Outputs:
- scaled: bfloat16 [2, 2, 4, 1024, 1024], P(None, 'freq', 'ma', 'pol', 'sky'), parts along dimension 4
- channel_power: float32 [4], P(('sky', 'freq')), parts along dimension 0
There are 2 independent parts, one for each index of `sky`. A program takes and returns all parts, laid end to end along the dimension named above; an argument that names none is the same for every part. Nothing has to cross between parts.
Inputs may be any that keep to these rules, and one draw needn't show every extreme that they name: `m_table`: the 4 values are distinct whole numbers below 512. `chan_mask`: at least one of the 2 channels is usable.
All inputs are finite; a program needn't handle non-finite values.
Results may differ from a plain program's by a relative error of at most 0.00055.
Values may be sent and summed in bfloat16 or wider, within the bound.
A program may use at most 64 MiB of HBM per device.

v0:
```python
import jax
import jax.numpy as jnp
from jax import lax
from jax.sharding import PartitionSpec as P


def on_device(alm, beam, m_table, chan_mask, noise):
    arrived = lax.all_to_all(alm, "ma", split_axis=3, concat_axis=2, tiled=True)
    blocks = arrived.reshape(
        arrived.shape[0],
        arrived.shape[1],
        lax.axis_size("ma"),
        arrived.shape[2] // lax.axis_size("ma"),
        arrived.shape[4],
    )
    joined = lax.all_gather(blocks, "pol", axis=3, tiled=True)
    coeffs_all = joined.reshape(
        joined.shape[0], joined.shape[1], joined.shape[2] * joined.shape[3], joined.shape[4]
    )
    degree = lax.iota(jnp.int32, coeffs_all.shape[2])
    keep_mask = (degree >= m_table[0])[None, None, :, None]
    coeffs = jnp.where(keep_mask, coeffs_all, jnp.zeros((), coeffs_all.dtype))
    response = beam[0]
    real_part = jnp.einsum(
        "fkl,fls->fks", response[:, 0], coeffs[0], preferred_element_type=jnp.float32
    ) - jnp.einsum("fkl,fls->fks", response[:, 1], coeffs[1], preferred_element_type=jnp.float32)
    imag_part = jnp.einsum(
        "fkl,fls->fks", response[:, 0], coeffs[1], preferred_element_type=jnp.float32
    ) + jnp.einsum("fkl,fls->fks", response[:, 1], coeffs[0], preferred_element_type=jnp.float32)
    visibility = jnp.stack([real_part, imag_part])
    weighted = visibility * visibility / noise[None, :, :, None]
    partial_power = jnp.sum(weighted, axis=(0, 2, 3))
    modes_total = jnp.float32(
        lax.axis_size("ma") * noise.shape[1] * lax.axis_size("pol") * visibility.shape[3]
    )
    mask_float = chan_mask.astype(jnp.float32)
    channel_power = lax.psum(partial_power, ("ma", "pol")) / modes_total
    masked_sum, live_count = lax.psum(
        (jnp.sum(mask_float * channel_power), jnp.sum(mask_float)), "freq"
    )
    band_power = masked_sum / live_count
    factor = mask_float / jnp.sqrt(0.5 * channel_power + 0.5 * band_power + 1e-06)
    scaled = visibility * (lax.rsqrt(noise) * factor[:, None])[None, :, :, None]
    return (scaled[:, :, None].astype(jnp.bfloat16), channel_power)


def solution(mesh):
    return jax.shard_map(
        on_device,
        mesh=mesh,
        in_specs=(
            P(None, "freq", ("ma", "pol"), None, "sky"),
            P("ma", "freq", None, "pol", None),
            P("ma"),
            P("freq"),
            P("freq", "pol"),
        ),
        out_specs=(P(None, "freq", "ma", "pol", "sky"), P(("sky", "freq"))),
        check_vma=False,
    )
```

profile of v0, /device:TPU:0, one launch (start us, length us, event | category | flops | bytes accessed | tf_op | source)
XLA Modules:
  0.0 94.6 jit_solution(7890521315917420241)
XLA Ops:
  7.2 0.0 all-gather.3.cloned.1.call-start
  7.2 1.4 %copy.10 = bf16[2,1,128,4,512]{4,2,0,1,3:T(8,128)(2,1)S(1)} copy(bf16[2,1,128,4,512]{4,3,2,1,0:T(4,128)(2,1)} %param.5) | data formatting | bytes 2097152 | tf_op args[0]
  8.6 31.9 %all_to_all.15 = bf16[2,1,128,4,512]{4,2,0,1,3:T(8,128)(2,1)S(1)} all-to-all(bf16[2,1,128,4,512]{4,2,0,1,3:T(8,128)(2,1)S(1)} %copy.10), channel_id=1, replica_groups=mesh['sky'=2,'ma'=4,'freq'=2,'pol'=2] {'ma'}, dimensions={3} | all-to-all | bytes 2097152 | tf_op jit(solution)/shard_map/all_to_all | solution.py:8
  40.5 1.1 %copy.14 = bf16[2,1,128,4,512]{4,2,3,0,1:T(8,128)(2,1)} copy(bf16[2,1,128,4,512]{4,2,0,1,3:T(8,128)(2,1)S(1)} %all_to_all.15) | data formatting | bytes 2097152 | tf_op jit(solution)/shard_map/all_to_all | solution.py:8
  41.6 0.0 all-gather.3.cloned.1.call-update
  42.9 8.5 %all-gather.3.cloned.1.call-done = bf16[2,1,4,256,1,512]{5,3,2,0,4,1:T(8,128)(2,1)} async-done(((bf16[2,1,4,128,1,512]{5,3,2,0,4,1:T(8,128)(2,1)}), bf16[2,1,4,256,1,512]{5,3,2,0,4,1:T(8,128)(2,1)}) %all-gather.3.cloned.1.call-update) | async-done | bytes 2097168 | tf_op jit(solution)/shard_map/all_gather | solution.py:16
  51.5 0.0 copy-start.1
  51.5 2.0 %broadcast_select_fusion = bf16[2,1,1024,512]{3,2,0,1:T(8,128)(2,1)S(1)} fusion(bf16[2,1,1024,512]{3,2,0,1:T(8,128)(2,1)} %bitcast.47, pred[1024]{0:T(1024)(128)(4,1)S(1)} %iota_compare_fusion), kind=kLoop, calls=%fused_computation.5 | loop fusion | flops 1048576 | bytes 4195328 | tf_op jit(solution)/shard_map/jit(_where)/select_n | solution.py:22
  53.4 0.3 copy-done.1
  53.7 0.7 fusion.3
  54.4 0.8 fusion.4
  55.2 0.8 convolution_subtract_fusion
  55.9 0.0 copy-start
  56.0 0.8 convolution_add_fusion
  56.7 0.0 copy-done
  56.7 1.1 %fusion.2 = f32[]{:T(128)} fusion(f32[1,1,512,512]{2,3,1,0:T(8,128)S(1)} %bitcast.45, f32[1,1,512,512]{2,3,1,0:T(8,128)S(1)} %bitcast.43, f32[512]{0:T(512)S(1)} %bitcast.48), kind=kLoop, calls=%fused_computation.4 | loop fusion | flops 2097151 | bytes 2099204 | tf_op jit(solution)/shard_map/reduce_sum | solution.py:32
  57.9 17.7 %psum.21 = f32[1]{0:T(128)} all-reduce(f32[1]{0:T(128)} %bitcast.16), channel_id=1, replica_groups=mesh['sky'=2,'ma'=4,'freq'=2,'pol'=2] {'ma','pol'}, use_global_device_ids=true, to_apply=%region_1.2 | all-reduce | flops 1 | bytes 8 | tf_op jit(solution)/shard_map/psum | solution.py:37
  76.9 6.7 %all-reduce = (f32[]{:T(128)}, f32[]{:T(128)}) all-reduce(f32[]{:T(128)} %bitcast.17, f32[]{:T(128)} %bitcast.18), channel_id=1, replica_groups=mesh['sky'=2,'ma'=4,'freq'=2,'pol'=2] {'freq'}, use_global_device_ids=true, to_apply=%region_2.3 | all-reduce | flops 2 | bytes 16 | tf_op jit(solution)/shard_map/psum | solution.py:38
  85.0 0.3 fusion
  85.3 1.3 %copy.12 = bf16[2,1,1,512,512]{4,3,2,1,0:T(8,128)(2,1)} copy(bf16[2,1,1,512,512]{3,4,2,1,0:T(8,128)(2,1)S(1)} %fusion) | data formatting | bytes 2097152
  (2 shorter events, 0.0 us)
Async XLA Ops:
  7.2 44.3 %all-gather.3.cloned.1.call-start = ((), (), s32[]{:S(2)}) async-start(), calls=%async_computation.1 | async-start | bytes 3145728 | tf_op jit(solution)/shard_map/all_gather | solution.py:16
  51.5 2.2 %copy-start.1 = (bf16[1,1,2,512,1024]{4,3,2,1,0:T(8,128)(2,1)S(1)}, bf16[1,1,2,512,1024]{4,3,2,1,0:T(8,128)(2,1)}, u32[]{:S(2)}) copy-start(bf16[1,1,2,512,1024]{4,3,2,1,0:T(8,128)(2,1)} %param.6) | copy-start | bytes 6291460
  55.9 0.8 copy-start
Sparse Core Ops, SparseCore 0:
  41.7 9.6 all-gather.2
where the time goes:
time: 94.9 us; the launch traced here: 94.6 us
  blocking collectives  56.3 us (59%)
  between operations  19.3 us (20%)
  waiting for transfers between devices  8.54 us (9%)
  local copies, waits for them, and re-layouts  4.09 us (4%)
  other arithmetic  3.39 us (4%)
  matrix products  3.01 us (3%)
    all_to_all x1, blocking collectives, on_device(): arrived = lax.all_to_all(alm, 'ma', split_axis=3, concat_axis=2, tiled=True)  31.9 us
    psum x1, blocking collectives, on_device(): channel_power = lax.psum(partial_power, ('ma', 'pol')) / modes_total  17.7 us
    all_gather x1, waiting for transfers between devices, on_device(): joined = lax.all_gather(blocks, 'pol', axis=3, tiled=True)  8.53 us
    psum x1, blocking collectives, on_device(): lax.psum((jnp.sum(mask_float * channel_power), jnp.sum(mask_float)), 'freq')  6.71 us
    unnamed x6, local copies, waits for them, and re-layouts  3.01 us
    select_n x1, other arithmetic, on_device(): coeffs = jnp.where(keep_mask, coeffs_all, jnp.zeros((), coeffs_all.dtype))  1.96 us
  transfers between devices with their start and end apart: 1, of which 1 were waited for; matrix products, arithmetic and copies ran while one was open for 0% of the time, Pallas kernels for 0%

commit v1 on v0

v1 whole, which is shorter than its diff:
```python
import functools

import jax
import jax.numpy as jnp
from jax import lax
from jax.experimental import pallas as pl
from jax.experimental.pallas import tpu as pltpu
from jax.sharding import PartitionSpec as P

MESH = pl.DeviceIdType.MESH


def near_first(n, me):
    if n > 8:
        shifts = [s for k in range(1, n // 2 + 1) for s in (k, n - k)][: n - 1]
        return [lax.rem(me + s, n) for s in shifts]
    table = [sorted((j for j in range(n) if j != i), key=lambda j: (abs(j - i), j)) for i in range(n)]
    order = []
    for k in range(n - 1):
        pick = jnp.int32(table[0][k])
        for i in range(1, n):
            pick = jnp.where(me == i, jnp.int32(table[i][k]), pick)
        order.append(pick)
    return order


def step_kernel(
    sizes, total, alm_ref, beam_ref, m_ref, mask_ref, noise_ref, out_ref, power_ref,
    recv, wide, acc, beam_v, inv_n, rs_n, mine, slots,
    z_send, z_recv, p_send, p_recv, own_sem, beam_sem, q_send, q_recv,
):
    n_ma, n_freq, n_pol = sizes
    n_all = n_ma * n_freq * n_pol
    ma, freq, pol = lax.axis_index("ma"), lax.axis_index("freq"), lax.axis_index("pol")
    block, columns = alm_ref.shape[2], alm_ref.shape[3]
    groups, _, rows, _ = recv.shape
    per_source = n_pol * block
    per_group = rows // per_source
    modes = beam_ref.shape[1]
    my_slot = (freq * n_ma + ma) * n_pol + pol

    def place(slot):
        return {"ma": lax.rem(slot // n_pol, n_ma), "freq": slot // (n_pol * n_ma), "pol": lax.rem(slot, n_pol)}

    def for_peers(body):
        if n_all <= 32:
            for r in range(1, n_all):
                body(r)
        else:
            lax.fori_loop(1, n_all, lambda r, _: (body(r), 0)[1], 0)

    beam_copy = pltpu.make_async_copy(beam_ref, beam_v, beam_sem)
    beam_copy.start()

    barrier = pltpu.get_barrier_semaphore()

    def greet(r):
        pl.semaphore_signal(barrier, inc=1, device_id=place(lax.rem(my_slot + r, n_all)), device_id_type=MESH)

    for_peers(greet)

    def part(source, core, c):
        start = lax.rem(source, per_group) * per_source + core * block
        return recv.at[source // per_group, c, pl.ds(pl.multiple_of(start, block), block)]

    own = [pltpu.make_async_copy(alm_ref.at[ma, c], part(ma, pol, c), own_sem.at[c]) for c in range(2)]
    for copy in own:
        copy.start()
    pl.semaphore_wait(barrier, n_all - 1)

    order = near_first(n_ma, ma)
    sends = []
    for k, dest in enumerate(order):
        for c in range(2):
            sends.append(pltpu.make_async_remote_copy(
                src_ref=alm_ref.at[dest, c], dst_ref=part(ma, pol, c),
                send_sem=z_send.at[k, c], recv_sem=z_recv.at[ma, c],
                device_id={"ma": dest}, device_id_type=MESH))
            sends[-1].start()

    def relay(source, c, src):
        hops = []
        for q in range(1, n_pol):
            hops.append(pltpu.make_async_remote_copy(
                src_ref=src, dst_ref=part(source, pol, c),
                send_sem=p_send.at[source, c], recv_sem=p_recv.at[source, c],
                device_id={"pol": lax.rem(pol + q, n_pol)}, device_id_type=MESH))
            hops[-1].start()
        return hops

    def arrival(source, c):
        return pltpu.make_async_remote_copy(
            src_ref=alm_ref.at[source, c], dst_ref=part(source, pol, c),
            send_sem=z_send.at[0, c], recv_sem=z_recv.at[source, c],
            device_id={"ma": source}, device_id_type=MESH)

    relays = [relay(ma, c, alm_ref.at[ma, c]) for c in range(2)]

    spread = jnp.transpose(jnp.broadcast_to(noise_ref[...], (128, modes)))
    inv_n[...] = 1.0 / spread
    rs_n[...] = lax.rsqrt(spread)
    mine[1:2, :] = jnp.full((1, 128), mask_ref[0].astype(jnp.float32))
    beam_copy.wait()
    strip = min(modes, 128)

    def widen(i, _):
        k0 = pl.multiple_of(i * strip, strip)
        for g in range(groups):
            degree = lax.broadcasted_iota(jnp.int32, (strip, rows), 1) + g * rows
            keep = degree >= m_ref[0]
            zero = jnp.zeros((strip, rows), jnp.float32)
            b0 = jnp.where(keep, beam_v[0, pl.ds(k0, strip), g * rows:(g + 1) * rows].astype(jnp.float32), zero)
            b1 = jnp.where(keep, beam_v[1, pl.ds(k0, strip), g * rows:(g + 1) * rows].astype(jnp.float32), zero)
            wide[g, 0, pl.ds(k0, strip), :] = b0.astype(wide.dtype)
            wide[g, 1, pl.ds(k0, strip), :] = (-b1).astype(wide.dtype)
            wide[g, 0, pl.ds(modes + k0, strip), :] = b1.astype(wide.dtype)
            wide[g, 1, pl.ds(modes + k0, strip), :] = b0.astype(wide.dtype)
        return 0

    lax.fori_loop(0, modes // strip, widen, 0)

    tile = min(modes, 256)
    tiles = 2 * modes // tile

    def accumulate(g, first):
        def body(i, _):
            k0 = pl.multiple_of(i * tile, tile)
            value = jnp.dot(wide[g, 0, pl.ds(k0, tile), :], recv[g, 0], preferred_element_type=jnp.float32)
            value += jnp.dot(wide[g, 1, pl.ds(k0, tile), :], recv[g, 1], preferred_element_type=jnp.float32)
            acc[pl.ds(k0, tile), :] = value if first else acc[pl.ds(k0, tile), :] + value
            return 0
        lax.fori_loop(0, tiles, body, 0)

    def squares(value, k0):
        noise_rows = inv_n[pl.ds(lax.rem(k0, modes), tile), :]
        sums = jnp.zeros((tile, 128), jnp.float32)
        for j in range(columns // 128):
            part_j = value[:, j * 128:(j + 1) * 128]
            sums += part_j * part_j
        return jnp.sum(sums * noise_rows, axis=0, keepdims=True)

    def finish(steps):
        def body(i, power):
            k0 = pl.multiple_of(i * tile, tile)
            value = acc[pl.ds(k0, tile), :]
            for g, c in steps:
                value += jnp.dot(wide[g, c, pl.ds(k0, tile), :], recv[g, c], preferred_element_type=jnp.float32)
            acc[pl.ds(k0, tile), :] = value
            return power + squares(value, k0)
        return lax.fori_loop(0, tiles, body, jnp.zeros((1, 128), jnp.float32))

    def add_half(g, c):
        def body(i, _):
            k0 = pl.multiple_of(i * tile, tile)
            acc[pl.ds(k0, tile), :] += jnp.dot(wide[g, c, pl.ds(k0, tile), :], recv[g, c], preferred_element_type=jnp.float32)
            return 0
        lax.fori_loop(0, tiles, body, 0)

    for copy in own:
        copy.wait()
    for c in range(2):
        for hop in relays[c]:
            hop.wait()
    if per_group == 1:
        accumulate(ma, True)
        for k, source in enumerate(order):
            later = []
            for c in range(2):
                arrival(source, c).wait_recv()
                later.append(relay(source, c, part(source, pol, c)))
            if k < len(order) - 1:
                for c in range(2):
                    for hop in later[c]:
                        hop.wait()
                accumulate(source, False)
            else:
                for hop in later[0]:
                    hop.wait()
                add_half(source, 0)
                for hop in later[1]:
                    hop.wait()
                power = finish([(source, 1)])
    else:
        later = []
        for source in order:
            for c in range(2):
                arrival(source, c).wait_recv()
                later.append(relay(source, c, part(source, pol, c)))
        for hops in later:
            for hop in hops:
                hop.wait()
        for g in range(groups):
            accumulate(g, g == 0)
        power = finish([])

    mine[0:1, :] = power
    slots[my_slot, 0:1, :] = power
    slots[my_slot, 1:2, :] = mine[1:2, :]

    def report(r):
        return pltpu.make_async_remote_copy(
            src_ref=mine, dst_ref=slots.at[my_slot], send_sem=q_send.at[r - 1], recv_sem=q_recv.at[my_slot],
            device_id=place(lax.rem(my_slot + r, n_all)), device_id_type=MESH)

    def heard(r):
        source = lax.rem(my_slot + r, n_all)
        pltpu.make_async_remote_copy(
            src_ref=mine, dst_ref=slots.at[source], send_sem=q_send.at[r - 1], recv_sem=q_recv.at[source],
            device_id=place(source), device_id_type=MESH).wait_recv()

    for_peers(lambda r: report(r).start())
    for copy in sends:
        copy.wait_send()
    for_peers(heard)

    per_freq = n_ma * n_pol
    masked, live, here = 0.0, 0.0, 0.0
    for f in range(n_freq):
        channel = jnp.sum(jnp.sum(slots[f * per_freq:(f + 1) * per_freq, 0, :], axis=0, keepdims=True), axis=1, keepdims=True) / total
        flag = slots[f * per_freq, 1:2, 0:1]
        masked += flag * channel
        live += flag
        here += jnp.where(freq == f, channel, 0.0)
    band = masked / live
    factor = mine[1:2, 0:1] / jnp.sqrt(0.5 * here + 0.5 * band + 1e-06)
    power_ref[0] = here[0, 0]

    def rescale(i, _):
        k0 = pl.multiple_of(i * strip, strip)
        scale = rs_n[pl.ds(k0, strip), :] * factor
        for c in range(2):
            for j in range(columns // 128):
                value = acc[pl.ds(c * modes + k0, strip), j * 128:(j + 1) * 128]
                out_ref[c, pl.ds(k0, strip), j * 128:(j + 1) * 128] = (value * scale).astype(out_ref.dtype)
        return 0

    lax.fori_loop(0, modes // strip, rescale, 0)
    for_peers(lambda r: report(r).wait_send())


def on_device(sizes, alm, beam, m_table, chan_mask, noise):
    n_ma, n_freq, n_pol = sizes
    planes = jnp.transpose(alm[:, 0], (2, 0, 1, 3))
    response = beam[0, 0]
    block, columns = planes.shape[2], planes.shape[3]
    modes, degrees = response.shape[1], response.shape[2]
    per_source = n_pol * block
    rows = per_source * max(1, min(n_ma, 256 // per_source))
    groups = degrees // rows
    n_all = n_ma * n_freq * n_pol
    total = float(n_ma * modes * n_pol * columns)
    vmem = pl.BlockSpec(memory_space=pltpu.VMEM)
    smem = pl.BlockSpec(memory_space=pltpu.SMEM)
    dma = pltpu.SemaphoreType.DMA
    scaled, power = pl.pallas_call(
        functools.partial(step_kernel, sizes, total),
        out_shape=(
            jax.ShapeDtypeStruct((2, modes, columns), jnp.bfloat16),
            jax.ShapeDtypeStruct((1,), jnp.float32),
        ),
        in_specs=[vmem, pl.BlockSpec(memory_space=pl.ANY), smem, smem, vmem],
        out_specs=(vmem, smem),
        scratch_shapes=[
            pltpu.VMEM((groups, 2, rows, columns), jnp.bfloat16),
            pltpu.VMEM((groups, 2, 2 * modes, rows), jnp.bfloat16),
            pltpu.VMEM((2 * modes, columns), jnp.float32),
            pltpu.VMEM((2, modes, degrees), jnp.bfloat16),
            pltpu.VMEM((modes, 128), jnp.float32),
            pltpu.VMEM((modes, 128), jnp.float32),
            pltpu.VMEM((2, 128), jnp.float32),
            pltpu.VMEM((n_all, 2, 128), jnp.float32),
            dma((n_ma, 2)), dma((n_ma, 2)), dma((n_ma, 2)), dma((n_ma, 2)), dma((2,)), dma,
            dma((n_all,)), dma((n_all,)),
        ],
        compiler_params=pltpu.CompilerParams(collective_id=0, has_side_effects=True, vmem_limit_bytes=40 * 1024 * 1024),
        name="driftscan_step",
    )(planes, response, m_table, chan_mask, noise)
    return scaled[:, None, None], power


def solution(mesh):
    sizes = (mesh.shape["ma"], mesh.shape["freq"], mesh.shape["pol"])
    return jax.shard_map(
        functools.partial(on_device, sizes),
        mesh=mesh,
        in_specs=(
            P(None, "freq", ("ma", "pol"), None, "sky"),
            P("ma", "freq", None, "pol", None),
            P("ma"),
            P("freq"),
            P("freq", "pol"),
        ),
        out_specs=(P(None, "freq", "ma", "pol", "sky"), P(("sky", "freq"))),
        check_vma=False,
    )
```

time: 94.9 us -> 47.8 us (0.50)
  blocking collectives: 56.3 us -> 0 us
  Pallas kernels: 0 us -> 41.3 us
  between operations: 19.3 us -> 3.88 us
  waiting for transfers between devices: 8.54 us -> 0 us
  other arithmetic: 3.39 us -> 0 us
  matrix products: 3.01 us -> 0 us
  local copies, waits for them, and re-layouts: 4.09 us -> 2.4 us
    pallas_call x0 -> x1, Pallas kernels: none -> 41.3 us  [on_device(): pl.pallas_call(functools.partial(step_kernel, sizes, total), out_shape=(j...]
    all_to_all x1 -> x0, blocking collectives: 31.9 us -> none  [on_device(): arrived = lax.all_to_all(alm, 'ma', split_axis=3, concat_axis=2, tiled=True)]
    psum x2 -> x0, blocking collectives: 24.4 us -> none  [the longest x1 17.7 us: on_device(): channel_power = lax.psum(partial_power, ('ma', 'pol')) / modes_total]
    all_gather x1 -> x0, waiting for transfers between devices: 8.53 us -> none  [on_device(): joined = lax.all_gather(blocks, 'pol', axis=3, tiled=True)]
    dot_general x4 -> x0, matrix products: 3.01 us -> none  [the longest x1 0.75 us: on_device(): jnp.einsum('fkl,fls->fks', response[:, 1], coeffs[0], preferred_element_t...]
    select_n x1 -> x0, other arithmetic: 1.96 us -> none  [on_device(): coeffs = jnp.where(keep_mask, coeffs_all, jnp.zeros((), coeffs_all.dtype))]
    reduce_sum x1 -> x0, other arithmetic: 1.14 us -> none  [on_device(): partial_power = jnp.sum(weighted, axis=(0, 2, 3))]
    all_to_all x1 -> x0, local copies, waits for them, and re-layouts: 1.08 us -> none  [on_device(): arrived = lax.all_to_all(alm, 'ma', split_axis=3, concat_axis=2, tiled=True)]
  transfers between devices with their start and end apart: 1 -> 0, of which waited for: 1 -> 0; matrix products, arithmetic and copies ran while one was open for 0% -> 0% of each run, Pallas kernels for 0% -> 0%
where the time goes in v1:
time: 47.8 us; the launch traced here: 47.6 us
  Pallas kernels  41.3 us (86%)
  between operations  3.88 us (8%)
  local copies, waits for them, and re-layouts  2.4 us (5%)
    pallas_call x1, Pallas kernels, on_device(): pl.pallas_call(functools.partial(step_kernel, sizes, total), out_shape=(j...  41.3 us
    unnamed x6, local copies, waits for them, and re-layouts  2.4 us

profile of v1, /device:TPU:0, one launch (start us, length us, event | category | flops | bytes accessed | tf_op | source)
XLA Modules:
  0.0 47.6 jit_solution(16197765804100203593)
XLA Ops:
  0.6 0.0 copy-start.1
  0.6 0.0 copy-start
  2.1 1.4 %copy.10 = bf16[2,1,128,4,512]{4,2,0,3,1:T(8,128)(2,1)S(1)} copy(bf16[2,1,128,4,512]{4,3,2,1,0:T(4,128)(2,1)} %param.5) | data formatting | bytes 2097152 | tf_op args[0]
  3.5 0.0 copy-done.1
  3.5 0.0 copy-done
  3.5 41.3 %driftscan_step.1 = (bf16[2,512,512]{2,1,0:T(8,128)(2,1)S(1)}, f32[1]{0:T(128)}) custom-call(bf16[4,2,128,512]{3,2,1,0:T(8,128)(2,1)S(1)} %bitcast.9, bf16[2,512,1024]{2,1,0:T(8,128)(2,1)S(1)} %bitcast.10, s32[1]{0:T(128)S(6)} %copy.13.m_ref, s32[1]{0:T(128)S(6)} %copy.14.mask_ref, f32[1,512]{1,0:T(1,128)S(1)} %copy-done.1), custom_call_target="tpu_custom_call" | custom-call | tf_op jit(solution)/shard_map/driftscan_step/pallas_call | solution.py:255
  44.9 1.0 %copy.15 = bf16[2,1,1,512,512]{4,3,2,1,0:T(8,128)(2,1)} copy(bf16[2,1,1,512,512]{4,3,2,1,0:T(8,128)(2,1)S(1)} %bitcast.11) | data formatting | bytes 2097152
Async XLA Ops:
  0.6 2.9 %copy-start.1 = (f32[1,512]{1,0:T(1,128)S(1)}, f32[1,512]{1,0:T(1,128)}, u32[]{:S(2)}) copy-start(f32[1,512]{1,0:T(1,128)} %noise_ref.1) | copy-start | bytes 6148
  0.6 2.9 %copy-start = (bf16[1,1,2,512,1024]{4,3,2,1,0:T(8,128)(2,1)S(1)}, bf16[1,1,2,512,1024]{4,3,2,1,0:T(8,128)(2,1)}, u32[]{:S(2)}) copy-start(bf16[1,1,2,512,1024]{4,3,2,1,0:T(8,128)(2,1)} %param.6) | copy-start | bytes 6291460

commit v2 on v1

--- a/solution.py
+++ b/solution.py
@@ -10,11 +10,20 @@
 MESH = pl.DeviceIdType.MESH
 
 
-def near_first(n, me):
+def arrival_order(n, i):
+    return sorted((j for j in range(n) if j != i), key=lambda j: (abs(j - i), j))
+
+
+def send_order(n, i):
+    order = sorted((j for j in range(n) if j != i), key=lambda j: (abs(j - i), (j > i) != (2 * i < n)))
+    return order[:1] + order[:0:-1] if i in (0, n - 1) else order
+
+
+def others(n, me, rule):
     if n > 8:
-        shifts = [s for k in range(1, n // 2 + 1) for s in (k, n - k)][: n - 1]
-        return [lax.rem(me + s, n) for s in shifts]
-    table = [sorted((j for j in range(n) if j != i), key=lambda j: (abs(j - i), j)) for i in range(n)]
+        ups = [jnp.where(me + s < n, me + s, n - 1 - s) for s in range(1, n)]
+        return ups
+    table = [rule(n, i) for i in range(n)]
     order = []
     for k in range(n - 1):
         pick = jnp.int32(table[0][k])
@@ -27,7 +36,7 @@
 def step_kernel(
     sizes, total, alm_ref, beam_ref, m_ref, mask_ref, noise_ref, out_ref, power_ref,
     recv, wide, acc, beam_v, inv_n, rs_n, mine, slots,
-    z_send, z_recv, p_send, p_recv, own_sem, beam_sem, q_send, q_recv,
+    z_send, z_recv, p_send, p_recv, own_sem, beam_sem, q_send, q_recv, chain, meet,
 ):
     n_ma, n_freq, n_pol = sizes
     n_all = n_ma * n_freq * n_pol
@@ -54,10 +63,23 @@
 
     barrier = pltpu.get_barrier_semaphore()
 
-    def greet(r):
-        pl.semaphore_signal(barrier, inc=1, device_id=place(lax.rem(my_slot + r, n_all)), device_id_type=MESH)
-
-    for_peers(greet)
+    def tell_line(sem):
+        @pl.when(ma > 0)
+        def _():
+            pl.semaphore_signal(sem, inc=1, device_id={"ma": ma - 1}, device_id_type=MESH)
+
+        @pl.when(ma < n_ma - 1)
+        def _():
+            pl.semaphore_signal(sem, inc=1, device_id={"ma": ma + 1}, device_id_type=MESH)
+
+    def tell(axis, me, n, sem):
+        for q in range(1, n):
+            pl.semaphore_signal(sem, inc=1, device_id={axis: lax.rem(me + q, n)}, device_id_type=MESH)
+
+    beside = jnp.where(ma > 0, 1, 0) + jnp.where(ma < n_ma - 1, 1, 0)
+    tell_line(barrier)
+    tell("pol", pol, n_pol, barrier)
+    tell("freq", freq, n_freq, barrier)
 
     def part(source, core, c):
         start = lax.rem(source, per_group) * per_source + core * block
@@ -66,17 +88,27 @@
     own = [pltpu.make_async_copy(alm_ref.at[ma, c], part(ma, pol, c), own_sem.at[c]) for c in range(2)]
     for copy in own:
         copy.start()
-    pl.semaphore_wait(barrier, n_all - 1)
-
-    order = near_first(n_ma, ma)
+    pl.semaphore_wait(barrier, beside + n_pol - 1 + n_freq - 1)
+
+    order = others(n_ma, ma, arrival_order)
+    targets = others(n_ma, ma, send_order)
     sends = []
-    for k, dest in enumerate(order):
+
+    def send(k):
         for c in range(2):
             sends.append(pltpu.make_async_remote_copy(
-                src_ref=alm_ref.at[dest, c], dst_ref=part(ma, pol, c),
+                src_ref=alm_ref.at[targets[k], c], dst_ref=part(ma, pol, c),
                 send_sem=z_send.at[k, c], recv_sem=z_recv.at[ma, c],
-                device_id={"ma": dest}, device_id_type=MESH))
+                device_id={"ma": targets[k]}, device_id_type=MESH))
             sends[-1].start()
+
+    if n_ma <= 8:
+        send(0)
+    for t in range(n_ma - 2):
+        tell_line(chain.at[t])
+        pl.semaphore_wait(chain.at[t], beside)
+    for k in range(len(sends) // 2, n_ma - 1):
+        send(k)
 
     def relay(source, c, src):
         hops = []
@@ -118,6 +150,10 @@
         return 0
 
     lax.fori_loop(0, modes // strip, widen, 0)
+    tell("pol", pol, n_pol, meet.at[0])
+    pl.semaphore_wait(meet.at[0], n_pol - 1)
+    tell("freq", freq, n_freq, meet.at[1])
+    pl.semaphore_wait(meet.at[1], n_freq - 1)
 
     tile = min(modes, 256)
     tiles = 2 * modes // tile
@@ -132,7 +168,7 @@
         lax.fori_loop(0, tiles, body, 0)
 
     def squares(value, k0):
-        noise_rows = inv_n[pl.ds(lax.rem(k0, modes), tile), :]
+        noise_rows = inv_n[k0 % modes:k0 % modes + tile, :]
         sums = jnp.zeros((tile, 128), jnp.float32)
         for j in range(columns // 128):
             part_j = value[:, j * 128:(j + 1) * 128]
@@ -140,21 +176,20 @@
         return jnp.sum(sums * noise_rows, axis=0, keepdims=True)
 
     def finish(steps):
-        def body(i, power):
-            k0 = pl.multiple_of(i * tile, tile)
-            value = acc[pl.ds(k0, tile), :]
+        power = jnp.zeros((1, 128), jnp.float32)
+        for i in range(tiles):
+            k0 = i * tile
+            value = acc[k0:k0 + tile, :]
             for g, c in steps:
-                value += jnp.dot(wide[g, c, pl.ds(k0, tile), :], recv[g, c], preferred_element_type=jnp.float32)
-            acc[pl.ds(k0, tile), :] = value
-            return power + squares(value, k0)
-        return lax.fori_loop(0, tiles, body, jnp.zeros((1, 128), jnp.float32))
+                value += jnp.dot(wide[g, c, k0:k0 + tile, :], recv[g, c], preferred_element_type=jnp.float32)
+            acc[k0:k0 + tile, :] = value
+            power += squares(value, k0)
+        return power
 
     def add_half(g, c):
-        def body(i, _):
-            k0 = pl.multiple_of(i * tile, tile)
-            acc[pl.ds(k0, tile), :] += jnp.dot(wide[g, c, pl.ds(k0, tile), :], recv[g, c], preferred_element_type=jnp.float32)
-            return 0
-        lax.fori_loop(0, tiles, body, 0)
+        for i in range(tiles):
+            k0 = i * tile
+            acc[k0:k0 + tile, :] += jnp.dot(wide[g, c, k0:k0 + tile, :], recv[g, c], preferred_element_type=jnp.float32)
 
     for copy in own:
         copy.wait()
@@ -271,6 +306,7 @@
             pltpu.VMEM((n_all, 2, 128), jnp.float32),
             dma((n_ma, 2)), dma((n_ma, 2)), dma((n_ma, 2)), dma((n_ma, 2)), dma((2,)), dma,
             dma((n_all,)), dma((n_all,)),
+            pltpu.SemaphoreType.REGULAR((max(1, n_ma - 2),)), pltpu.SemaphoreType.REGULAR((2,)),
         ],
         compiler_params=pltpu.CompilerParams(collective_id=0, has_side_effects=True, vmem_limit_bytes=40 * 1024 * 1024),
         name="driftscan_step",

time: 47.8 us -> 44.8 us (0.937)
  Pallas kernels: 41.3 us -> 38.3 us
    pallas_call x1, Pallas kernels: 41.3 us -> 38.3 us  [on_device(): pl.pallas_call(functools.partial(step_kernel, sizes, total), out_shape=(j...]
where the time goes in v2:
time: 44.8 us; the launch traced here: 44.6 us
  Pallas kernels  38.3 us (85%)
  between operations  3.88 us (9%)
  local copies, waits for them, and re-layouts  2.4 us (5%)
    pallas_call x1, Pallas kernels, on_device(): pl.pallas_call(functools.partial(step_kernel, sizes, total), out_shape=(j...  38.3 us
    unnamed x6, local copies, waits for them, and re-layouts  2.4 us

profile of v2, /device:TPU:0, one launch (start us, length us, event | category | flops | bytes accessed | tf_op | source)
XLA Modules:
  0.0 44.6 jit_solution(4278142203195078003)
XLA Ops:
  0.6 0.0 copy-start.1
  0.6 0.0 copy-start
  2.1 1.4 %copy.10 = bf16[2,1,128,4,512]{4,2,0,3,1:T(8,128)(2,1)S(1)} copy(bf16[2,1,128,4,512]{4,3,2,1,0:T(4,128)(2,1)} %param.5) | data formatting | bytes 2097152 | tf_op args[0]
  3.5 0.0 copy-done.1
  3.5 0.0 copy-done
  3.5 38.3 %driftscan_step.1 = (bf16[2,512,512]{2,1,0:T(8,128)(2,1)S(1)}, f32[1]{0:T(128)}) custom-call(bf16[4,2,128,512]{3,2,1,0:T(8,128)(2,1)S(1)} %bitcast.9, bf16[2,512,1024]{2,1,0:T(8,128)(2,1)S(1)} %bitcast.10, s32[1]{0:T(128)S(6)} %copy.13.m_ref, s32[1]{0:T(128)S(6)} %copy.14.mask_ref, f32[1,512]{1,0:T(1,128)S(1)} %copy-done.1), custom_call_target="tpu_custom_call" | custom-call | tf_op jit(solution)/shard_map/driftscan_step/pallas_call | solution.py:290
  41.9 1.0 %copy.15 = bf16[2,1,1,512,512]{4,3,2,1,0:T(8,128)(2,1)} copy(bf16[2,1,1,512,512]{4,3,2,1,0:T(8,128)(2,1)S(1)} %bitcast.11) | data formatting | bytes 2097152
Async XLA Ops:
  0.6 2.9 %copy-start.1 = (f32[1,512]{1,0:T(1,128)S(1)}, f32[1,512]{1,0:T(1,128)}, u32[]{:S(2)}) copy-start(f32[1,512]{1,0:T(1,128)} %noise_ref.1) | copy-start | bytes 6148
  0.6 2.9 %copy-start = (bf16[1,1,2,512,1024]{4,3,2,1,0:T(8,128)(2,1)S(1)}, bf16[1,1,2,512,1024]{4,3,2,1,0:T(8,128)(2,1)}, u32[]{:S(2)}) copy-start(bf16[1,1,2,512,1024]{4,3,2,1,0:T(8,128)(2,1)} %param.6) | copy-start | bytes 6291460

commit v3 on v2

--- a/solution.py
+++ b/solution.py
@@ -34,9 +34,9 @@
 
 
 def step_kernel(
-    sizes, total, alm_ref, beam_ref, m_ref, mask_ref, noise_ref, out_ref, power_ref,
-    recv, wide, acc, beam_v, inv_n, rs_n, mine, slots,
-    z_send, z_recv, p_send, p_recv, own_sem, beam_sem, q_send, q_recv, chain, meet,
+    sizes, total, alm_ref, beam_ref, m_hbm, mask_hbm, noise_hbm, acc, scale_ref, power_ref,
+    recv, wide, beam_v, inv_n, rs_n, mine, slots, m_ref, mask_ref, noise_ref,
+    z_send, z_recv, p_send, p_recv, own_sem, beam_sem, q_send, q_recv, chain, meet, small_sem,
 ):
     n_ma, n_freq, n_pol = sizes
     n_all = n_ma * n_freq * n_pol
@@ -60,6 +60,12 @@
 
     beam_copy = pltpu.make_async_copy(beam_ref, beam_v, beam_sem)
     beam_copy.start()
+    small = [
+        pltpu.make_async_copy(src, dst, small_sem.at[i])
+        for i, (src, dst) in enumerate(((m_hbm, m_ref), (mask_hbm, mask_ref), (noise_hbm, noise_ref)))
+    ]
+    for copy in small:
+        copy.start()
 
     barrier = pltpu.get_barrier_semaphore()
 
@@ -128,6 +134,8 @@
 
     relays = [relay(ma, c, alm_ref.at[ma, c]) for c in range(2)]
 
+    for copy in small:
+        copy.wait()
     spread = jnp.transpose(jnp.broadcast_to(noise_ref[...], (128, modes)))
     inv_n[...] = 1.0 / spread
     rs_n[...] = lax.rsqrt(spread)
@@ -258,19 +266,29 @@
         here += jnp.where(freq == f, channel, 0.0)
     band = masked / live
     factor = mine[1:2, 0:1] / jnp.sqrt(0.5 * here + 0.5 * band + 1e-06)
-    power_ref[0] = here[0, 0]
-
-    def rescale(i, _):
-        k0 = pl.multiple_of(i * strip, strip)
-        scale = rs_n[pl.ds(k0, strip), :] * factor
+    power_ref[...] = jnp.broadcast_to(here, power_ref.shape)
+    scale_ref[...] = rs_n[...] * factor
+    for_peers(lambda r: report(r).wait_send())
+
+
+def rescale_kernel(acc, scale_ref, power_ref, out_ref, channel_ref, staged, sems):
+    modes = scale_ref.shape[0]
+    columns = acc.shape[1]
+    strip = modes // sems.shape[0]
+    channel_ref[0] = power_ref[0, 0]
+    copies = []
+    for i in range(sems.shape[0]):
+        k0 = i * strip
+        scale = scale_ref[k0:k0 + strip, :]
         for c in range(2):
             for j in range(columns // 128):
-                value = acc[pl.ds(c * modes + k0, strip), j * 128:(j + 1) * 128]
-                out_ref[c, pl.ds(k0, strip), j * 128:(j + 1) * 128] = (value * scale).astype(out_ref.dtype)
-        return 0
-
-    lax.fori_loop(0, modes // strip, rescale, 0)
-    for_peers(lambda r: report(r).wait_send())
+                value = acc[c * modes + k0:c * modes + k0 + strip, j * 128:(j + 1) * 128]
+                staged[c, k0:k0 + strip, j * 128:(j + 1) * 128] = (value * scale).astype(staged.dtype)
+        copies.append(pltpu.make_async_copy(
+            staged.at[:, pl.ds(k0, strip)], out_ref.at[:, pl.ds(k0, strip)], sems.at[i]))
+        copies[-1].start()
+    for copy in copies:
+        copy.wait()
 
 
 def on_device(sizes, alm, beam, m_table, chan_mask, noise):
@@ -287,31 +305,48 @@
     vmem = pl.BlockSpec(memory_space=pltpu.VMEM)
     smem = pl.BlockSpec(memory_space=pltpu.SMEM)
     dma = pltpu.SemaphoreType.DMA
-    scaled, power = pl.pallas_call(
+    hbm = pl.BlockSpec(memory_space=pl.ANY)
+    visibility, scale, power = pl.pallas_call(
         functools.partial(step_kernel, sizes, total),
         out_shape=(
-            jax.ShapeDtypeStruct((2, modes, columns), jnp.bfloat16),
-            jax.ShapeDtypeStruct((1,), jnp.float32),
+            jax.ShapeDtypeStruct((2 * modes, columns), jnp.float32),
+            jax.ShapeDtypeStruct((modes, 128), jnp.float32),
+            jax.ShapeDtypeStruct((1, 128), jnp.float32),
         ),
-        in_specs=[vmem, pl.BlockSpec(memory_space=pl.ANY), smem, smem, vmem],
-        out_specs=(vmem, smem),
+        in_specs=[vmem, hbm, hbm, hbm, hbm],
+        out_specs=(vmem, vmem, vmem),
         scratch_shapes=[
             pltpu.VMEM((groups, 2, rows, columns), jnp.bfloat16),
             pltpu.VMEM((groups, 2, 2 * modes, rows), jnp.bfloat16),
-            pltpu.VMEM((2 * modes, columns), jnp.float32),
             pltpu.VMEM((2, modes, degrees), jnp.bfloat16),
             pltpu.VMEM((modes, 128), jnp.float32),
             pltpu.VMEM((modes, 128), jnp.float32),
             pltpu.VMEM((2, 128), jnp.float32),
             pltpu.VMEM((n_all, 2, 128), jnp.float32),
+            pltpu.SMEM((1,), jnp.int32),
+            pltpu.SMEM((1,), jnp.int32),
+            pltpu.VMEM((1, modes), jnp.float32),
             dma((n_ma, 2)), dma((n_ma, 2)), dma((n_ma, 2)), dma((n_ma, 2)), dma((2,)), dma,
             dma((n_all,)), dma((n_all,)),
-            pltpu.SemaphoreType.REGULAR((max(1, n_ma - 2),)), pltpu.SemaphoreType.REGULAR((2,)),
+            pltpu.SemaphoreType.REGULAR((max(1, n_ma - 2),)), pltpu.SemaphoreType.REGULAR((2,)), dma((3,)),
         ],
         compiler_params=pltpu.CompilerParams(collective_id=0, has_side_effects=True, vmem_limit_bytes=40 * 1024 * 1024),
         name="driftscan_step",
     )(planes, response, m_table, chan_mask, noise)
-    return scaled[:, None, None], power
+    pieces = 4 if modes % 64 == 0 else 1
+    scaled, channel_power = pl.pallas_call(
+        rescale_kernel,
+        out_shape=(
+            jax.ShapeDtypeStruct((2, modes, columns), jnp.bfloat16),
+            jax.ShapeDtypeStruct((1,), jnp.float32),
+        ),
+        in_specs=[vmem, vmem, vmem],
+        out_specs=(hbm, smem),
+        scratch_shapes=[pltpu.VMEM((2, modes, columns), jnp.bfloat16), dma((pieces,))],
+        compiler_params=pltpu.CompilerParams(vmem_limit_bytes=16 * 1024 * 1024),
+        name="rescale",
+    )(visibility, scale, power)
+    return scaled[:, None, None], channel_power
 
 
 def solution(mesh):

time: 44.8 us -> 42.9 us (0.958)
  between operations: 3.88 us -> 2.12 us
  local copies, waits for them, and re-layouts: 2.4 us -> 1.43 us
  Pallas kernels: 38.3 us -> 39.2 us
    pallas_call x0 -> x1, Pallas kernels: none -> 1.57 us  [on_device(): pl.pallas_call(rescale_kernel, out_shape=(jax.ShapeDtypeStruct((2, modes,...]
    unnamed x6 -> x5, local copies, waits for them, and re-layouts: 2.4 us -> 1.43 us
    pallas_call x1, Pallas kernels: 38.3 us -> 37.6 us  [on_device(): pl.pallas_call(functools.partial(step_kernel, sizes, total), out_shape=(j...]
where the time goes in v3:
time: 42.9 us; the launch traced here: 42.7 us
  Pallas kernels  39.2 us (91%)
  between operations  2.12 us (5%)
  local copies, waits for them, and re-layouts  1.43 us (3%)
    pallas_call x1, Pallas kernels, on_device(): pl.pallas_call(functools.partial(step_kernel, sizes, total), out_shape=(j...  37.6 us
    pallas_call x1, Pallas kernels, on_device(): pl.pallas_call(rescale_kernel, out_shape=(jax.ShapeDtypeStruct((2, modes,...  1.57 us
    unnamed x5, local copies, waits for them, and re-layouts  1.43 us

profile of v3, /device:TPU:0, one launch (start us, length us, event | category | flops | bytes accessed | tf_op | source)
XLA Modules:
  0.0 42.7 jit_solution(17411548995884129618)
XLA Ops:
  0.6 0.0 copy-start.1
  0.6 0.0 copy-start
  2.1 1.4 %copy.10 = bf16[2,1,128,4,512]{4,2,0,3,1:T(8,128)(2,1)S(1)} copy(bf16[2,1,128,4,512]{4,3,2,1,0:T(4,128)(2,1)} %param.5) | data formatting | bytes 2097152 | tf_op args[0]
  3.5 0.0 copy-done.1
  3.5 0.0 copy-done
  3.5 37.6 %driftscan_step.1 = (f32[1024,512]{1,0:T(8,128)S(1)}, f32[512,128]{1,0:T(8,128)S(1)}, f32[1,128]{1,0:T(1,128)S(1)}) custom-call(bf16[4,2,128,512]{3,2,1,0:T(8,128)(2,1)S(1)} %bitcast.9, bf16[2,512,1024]{2,1,0:T(8,128)(2,1)S(1)} %bitcast.10, s32[1]{0:T(128)S(6)} %copy.11.m_hbm, s32[1]{0:T(128)S(6)} %copy.12.mask_hbm, f32[1,512]{1,0:T(1,128)S(1)} %copy-done.1), custom_call_target="tpu_custom_call" | custom-call | tf_op jit(solution)/shard_map/driftscan_step/pallas_call | solution.py:309
  41.1 1.6 %rescale.1 = (bf16[2,512,512]{2,1,0:T(8,128)(2,1)}, f32[1]{0:T(128)}) custom-call(f32[1024,512]{1,0:T(8,128)S(1)} %get-tuple-element.7.acc, f32[512,128]{1,0:T(8,128)S(1)} %get-tuple-element.8.scale_ref, f32[1,128]{1,0:T(1,128)S(1)} %get-tuple-element.9.power_ref), custom_call_target="tpu_custom_call" | custom-call | tf_op jit(solution)/shard_map/rescale/pallas_call | solution.py:337
Async XLA Ops:
  0.6 2.9 %copy-start.1 = (f32[1,512]{1,0:T(1,128)S(1)}, f32[1,512]{1,0:T(1,128)}, u32[]{:S(2)}) copy-start(f32[1,512]{1,0:T(1,128)} %noise_hbm.1) | copy-start | bytes 6148
  0.6 2.9 %copy-start = (bf16[1,1,2,512,1024]{4,3,2,1,0:T(8,128)(2,1)S(1)}, bf16[1,1,2,512,1024]{4,3,2,1,0:T(8,128)(2,1)}, u32[]{:S(2)}) copy-start(bf16[1,1,2,512,1024]{4,3,2,1,0:T(8,128)(2,1)} %param.6) | copy-start | bytes 6291460

commit v4 on v3

--- a/solution.py
+++ b/solution.py
@@ -163,7 +163,7 @@
     tell("freq", freq, n_freq, meet.at[1])
     pl.semaphore_wait(meet.at[1], n_freq - 1)
 
-    tile = min(modes, 256)
+    tile = min(modes, 512)
     tiles = 2 * modes // tile
 
     def accumulate(g, first):

time: 42.9 us -> 42.5 us (level)
  no operation moved by 1% of the time
where the time goes in v4:
time: 42.5 us; the launch traced here: 42.4 us
  Pallas kernels  38.8 us (91%)
  between operations  2.12 us (5%)
  local copies, waits for them, and re-layouts  1.43 us (3%)
    pallas_call x1, Pallas kernels, on_device(): pl.pallas_call(functools.partial(step_kernel, sizes, total), out_shape=(j...  37.3 us
    pallas_call x1, Pallas kernels, on_device(): pl.pallas_call(rescale_kernel, out_shape=(jax.ShapeDtypeStruct((2, modes,...  1.57 us
    unnamed x5, local copies, waits for them, and re-layouts  1.43 us

profile of v4, /device:TPU:0, one launch (start us, length us, event | category | flops | bytes accessed | tf_op | source)
XLA Modules:
  0.0 42.4 jit_solution(7920503400327475124)
XLA Ops:
  0.6 0.0 copy-start.1
  0.6 0.0 copy-start
  2.1 1.4 %copy.10 = bf16[2,1,128,4,512]{4,2,0,3,1:T(8,128)(2,1)S(1)} copy(bf16[2,1,128,4,512]{4,3,2,1,0:T(4,128)(2,1)} %param.5) | data formatting | bytes 2097152 | tf_op args[0]
  3.5 0.0 copy-done.1
  3.5 0.0 copy-done
  3.5 37.3 %driftscan_step.1 = (f32[1024,512]{1,0:T(8,128)S(1)}, f32[512,128]{1,0:T(8,128)S(1)}, f32[1,128]{1,0:T(1,128)S(1)}) custom-call(bf16[4,2,128,512]{3,2,1,0:T(8,128)(2,1)S(1)} %bitcast.9, bf16[2,512,1024]{2,1,0:T(8,128)(2,1)S(1)} %bitcast.10, s32[1]{0:T(128)S(6)} %copy.11.m_hbm, s32[1]{0:T(128)S(6)} %copy.12.mask_hbm, f32[1,512]{1,0:T(1,128)S(1)} %copy-done.1), custom_call_target="tpu_custom_call" | custom-call | tf_op jit(solution)/shard_map/driftscan_step/pallas_call | solution.py:309
  40.8 1.6 %rescale.1 = (bf16[2,512,512]{2,1,0:T(8,128)(2,1)}, f32[1]{0:T(128)}) custom-call(f32[1024,512]{1,0:T(8,128)S(1)} %get-tuple-element.7.acc, f32[512,128]{1,0:T(8,128)S(1)} %get-tuple-element.8.scale_ref, f32[1,128]{1,0:T(1,128)S(1)} %get-tuple-element.9.power_ref), custom_call_target="tpu_custom_call" | custom-call | tf_op jit(solution)/shard_map/rescale/pallas_call | solution.py:337
Async XLA Ops:
  0.6 2.9 %copy-start.1 = (f32[1,512]{1,0:T(1,128)S(1)}, f32[1,512]{1,0:T(1,128)}, u32[]{:S(2)}) copy-start(f32[1,512]{1,0:T(1,128)} %noise_hbm.1) | copy-start | bytes 6148
  0.6 2.9 %copy-start = (bf16[1,1,2,512,1024]{4,3,2,1,0:T(8,128)(2,1)S(1)}, bf16[1,1,2,512,1024]{4,3,2,1,0:T(8,128)(2,1)}, u32[]{:S(2)}) copy-start(bf16[1,1,2,512,1024]{4,3,2,1,0:T(8,128)(2,1)} %param.6) | copy-start | bytes 6291460
